TPU v7x, 32 devices: a whole 2x2x4 slice. The times are simulated.
32 devices in a mesh: seq: 8 (over z, x), head: 4 (over y, core).
Axes of the slice: x: 2, y: 2, z: 4, core: 2. Of those that a mesh axis runs over, the one named last changes fastest.
Arguments:
- tokens: bfloat16 [2048, 4608], P('seq', 'head'), may hold values from -32 to 32
- segments: int32 [2048], P('seq'), may hold values from 0 to 7, never falling along the last dimension, each value on 1 to 1024 neighbouring positions
- pre_gain: float32 [4608], replicated, may hold values from 0.1 to 1.9
- post_gain: float32 [4608], replicated, may hold values from 0.1 to 1.9
- w_query: bfloat16 [4608, 1024], P('seq', 'head'), may hold values from -0.375 to 0.375
- w_key: bfloat16 [4608, 512], P('seq', 'head'), may hold values from -0.1875 to 0.1875
- w_value: bfloat16 [4608, 512], P('seq', 'head'), may hold values from -0.09375 to 0.09375
- w_out: bfloat16 [1024, 4608], P('head', 'seq'), may hold values from -0.1875 to 0.1875
Outputs:
- mixed: bfloat16 [2048, 4608], P('seq')
Inputs may be any that keep to these rules, and one draw needn't show every extreme that they name: `segments`: segment ids never fall; each of the 8 documents holds at least one token and at most 1024, one exactly 1024.
All inputs are finite; a program needn't handle non-finite values.
Results may differ from a plain program's by a relative error of at most 0.01.
Values may be sent and summed in bfloat16 or wider, within the bound.
A program may use at most 64 MiB of HBM per device.

v0:
```python
import jax
import jax.numpy as jnp
from jax import lax
from jax.sharding import PartitionSpec as P

HD = 128
GROUP = 2
SCALAR = 144
DOCS = 8
EPS = 1e-06
CAP = 50.0


def carried_in(value, axis, join, neutral):
    count, mine = (lax.axis_size(axis), lax.axis_index(axis))
    pieces = lax.all_gather(value, axis)
    subtotal = jnp.full_like(value, 0) + jnp.asarray(neutral, value.dtype)

    def step(position, subtotal):
        longer = join(subtotal, pieces[position])
        return jnp.where(position < mine, longer, subtotal)

    return lax.fori_loop(0, count - 1, step, subtotal)


def rotate(values, position, width):
    count = values.shape[1] // width
    half = width // 2
    shaped = values.reshape(values.shape[0], count, width)
    freq = 10000.0 ** (-(jnp.arange(half, dtype=jnp.float32) / half))
    angle = position[:, None] * freq[None, :]
    cosine = jnp.cos(angle)[:, None, :]
    sine = jnp.sin(angle)[:, None, :]
    first = shaped[:, :, :half]
    second = shaped[:, :, half:]
    turned = jnp.concatenate(
        [first * cosine - second * sine, second * cosine + first * sine], axis=2
    )
    return turned.reshape(values.shape[0], count * width)


def add_counts(earlier, later):
    return earlier + later


def local(tokens, segments, pre_gain, post_gain, w_query, w_key, w_value, w_out):
    rows = tokens.shape[0]
    whole = lax.all_gather(tokens, "head", axis=1, tiled=True)
    wide = whole.astype(jnp.float32)
    normed = (
        wide * lax.rsqrt(jnp.mean(wide * wide, axis=1, keepdims=True) + EPS) * pre_gain
    ).astype(jnp.bfloat16)
    pieces = (
        lax.all_gather(w_query, "seq", axis=0, tiled=True),
        lax.all_gather(w_key, "seq", axis=0, tiled=True),
        lax.all_gather(w_value, "seq", axis=0, tiled=True),
    )
    query, key_proj, value_proj = tuple(
        (jnp.dot(normed, piece, preferred_element_type=jnp.float32) for piece in pieces)
    )
    levels = jnp.arange(DOCS, dtype=jnp.int32)
    below = jnp.sum((levels[None, :] > segments[:, None]).astype(jnp.float32), axis=0)
    earlier = carried_in(below, "seq", add_counts, jnp.zeros((DOCS,), jnp.float32))
    starts = earlier + below
    onehot = (segments[:, None] == levels[None, :]).astype(jnp.float32)
    tok_start = jnp.sum(onehot * starts[None, :], axis=1)
    offset = lax.axis_index("seq") * rows
    index_f = (offset + jnp.arange(rows, dtype=jnp.int32)).astype(jnp.float32)
    position = index_f - tok_start
    kv_count = w_key.shape[1] // HD
    rq = (rotate(query, position, HD) * SCALAR ** (-0.5)).astype(jnp.bfloat16)
    rk = rotate(key_proj, position, HD).astype(jnp.bfloat16)
    vb = value_proj.astype(jnp.bfloat16)
    stacked = (
        rq.reshape(rows, kv_count, GROUP, HD)
        .transpose(1, 2, 0, 3)
        .reshape(kv_count, GROUP * rows, HD)
    )
    query_start = jnp.tile(tok_start, GROUP)
    query_index = jnp.tile(index_f, GROUP)
    empty = (
        jnp.zeros((kv_count, GROUP * rows, HD), jnp.float32),
        jnp.zeros((kv_count, GROUP * rows), jnp.float32),
    )
    keys_all = lax.all_gather(rk, "seq", axis=0, tiled=True)
    values_all = lax.all_gather(vb, "seq", axis=0, tiled=True)
    count = keys_all.shape[0]
    block = 1024
    steps_total = count // block

    def compute(offset_blk, state):
        numer, denom = state
        keys_blk = lax.dynamic_slice_in_dim(keys_all, offset_blk, block, 0).reshape(
            block, kv_count, HD
        )
        values_blk = lax.dynamic_slice_in_dim(values_all, offset_blk, block, 0).reshape(
            block, kv_count, HD
        )
        key_index = (offset_blk + jnp.arange(block, dtype=jnp.int32)).astype(jnp.float32)
        scores = jnp.einsum("cqd,kcd->cqk", stacked, keys_blk, preferred_element_type=jnp.float32)
        capped = CAP * jnp.tanh(scores / CAP)
        allowed = (key_index[None, None, :] >= query_start[None, :, None]) & (
            key_index[None, None, :] <= query_index[None, :, None]
        )
        weights = jnp.where(allowed, jnp.exp(capped), 0.0)
        numer = numer + jnp.einsum(
            "cqk,kcd->cqd",
            weights.astype(jnp.bfloat16),
            values_blk,
            preferred_element_type=jnp.float32,
        )
        denom = denom + jnp.sum(weights, axis=2)
        return (numer, denom)

    def one_block(step, state):
        offset_blk = step * block
        return compute(offset_blk, state)

    numer, denom = lax.fori_loop(0, steps_total, one_block, empty)
    attn = (numer / denom[:, :, None]).reshape(kv_count, GROUP, rows, HD).transpose(2, 0, 1, 3)
    attn = attn.reshape(rows, kv_count * GROUP * HD).astype(jnp.bfloat16)
    partial_proj = jnp.dot(
        attn, lax.all_gather(w_out, "seq", axis=1, tiled=True), preferred_element_type=jnp.float32
    )
    partial_proj = lax.optimization_barrier(partial_proj.astype(jnp.bfloat16)).astype(jnp.float32)
    summed = lax.psum(partial_proj.astype(jnp.bfloat16), "head").astype(jnp.float32)
    scale = lax.rsqrt(jnp.mean(summed * summed, axis=1, keepdims=True) + EPS)
    return (wide + summed * scale * post_gain).astype(jnp.bfloat16)


def solution(mesh):
    return jax.shard_map(
        local,
        mesh=mesh,
        in_specs=(
            P("seq", "head"),
            P("seq"),
            P(),
            P(),
            P("seq", "head"),
            P("seq", "head"),
            P("seq", "head"),
            P("head", "seq"),
        ),
        out_specs=P("seq", None),
        check_vma=False,
    )
```

profile of v0, /device:TPU:0, one launch (start us, length us, event | category | flops | bytes accessed | tf_op | source)
XLA Modules:
  0.0 300.0 jit_solution(1061354986700771852)
XLA Ops:
  6.5 0.7 all-gather.8.cloned.1.call-update
  7.3 0.7 all-gather.10.cloned.1.call-update
  8.1 0.7 all-gather.14.cloned.1.call-update
  10.0 0.8 convert_reduce_fusion
  10.8 1.3 dynamic-slice
  12.9 23.1 %all-reduce = f32[64]{0:T(128)S(1)} all-reduce(f32[64]{0:T(128)S(1)} %dynamic-update-slice), channel_id=2, replica_groups=mesh['seq'=8,'head'=4] {'seq'}, use_global_device_ids=true, to_apply=%add | all-reduce | flops 64 | bytes 512
  36.4 0.8 select_reduce_fusion
  37.5 2.4 fusion.14
  39.9 39.1 %all-gather.10.cloned.1.call-done = bf16[4608,128]{1,0:T(8,128)(2,1)} async-done(((bf16[576,128]{1,0:T(8,128)(2,1)}), bf16[4608,128]{1,0:T(8,128)(2,1)}) %all-gather.10.cloned.1.call-update) | async-done | bytes 1179664 | tf_op jit(solution)/shard_map/all_gather | solution.py:55
  79.0 2.3 convolution_bitcast_fusion.1
  81.7 34.4 %all-gather.1 = bf16[2048,1,128]{0,2,1:T(8,128)(2,1)} all-gather(bf16[256,1,128]{0,2,1:T(8,128)(2,1)S(1)} %pad_maximum_fusion), channel_id=3, replica_groups=mesh['seq'=8,'head'=4] {'seq'}, dimensions={0}, use_global_device_ids=true | all-gather | bytes 589824 | tf_op jit(solution)/shard_map/all_gather | solution.py:85
  116.1 6.3 %all-gather.14.cloned.1.call-done = bf16[4608,128]{1,0:T(8,128)(2,1)} async-done(((bf16[576,128]{1,0:T(8,128)(2,1)}), bf16[4608,128]{1,0:T(8,128)(2,1)}) %all-gather.14.cloned.1.call-update) | async-done | bytes 1179664 | tf_op jit(solution)/shard_map/all_gather | solution.py:56
  122.4 2.2 convolution_convert_fusion.1
  124.6 32.3 %all_gather.34 = bf16[2048,128]{1,0:T(8,128)(2,1)S(1)} all-gather(bf16[256,128]{1,0:T(8,128)(2,1)S(1)} %convolution_convert_fusion.1), channel_id=1, replica_groups=mesh['seq'=8,'head'=4] {'seq'}, dimensions={0}, use_global_device_ids=true | all-gather | bytes 589824 | tf_op jit(solution)/shard_map/all_gather | solution.py:86
  156.9 20.0 %all-gather.12.cloned.1.call-done = bf16[4608,256]{1,0:T(8,128)(2,1)} async-done(((bf16[576,256]{1,0:T(8,128)(2,1)}), bf16[4608,256]{1,0:T(8,128)(2,1)}) %all-gather.12.cloned.1.call-update) | async-done | bytes 2359312 | tf_op jit(solution)/shard_map/all_gather | solution.py:54
  177.0 3.0 fusion.30
  180.1 5.0 %while.31 = (s32[]{:T(128)}, f32[1,512,128]{2,1,0:T(8,128)S(1)}, f32[1,512]{1,0:T(1,128)S(1)}, bf16[2048,128]{0,1:T(8,128)(2,1)}, bf16[1,512,128]{2,1,0:T(8,128)...) while((s32[]{:T(128)}, f32[1,512,128]{2,1,0:T(8,128)S(1)}, ...), condition=%wide.region_7.8_spmd.clone, body=%wide.region_5.7_spmd.clone.sunk | while | flops 272763392 | bytes 3311802 | solution.py:119
  180.2 1.9 fusion.47
  182.7 1.9 fusion.47
  185.4 44.5 %all-gather.16.cloned.1.call-done = bf16[256,4608]{0,1:T(8,128)(2,1)} async-done(((bf16[256,576]{0,1:T(8,128)(2,1)}), bf16[256,4608]{0,1:T(8,128)(2,1)}) %all-gather.16.cloned.1.call-update) | async-done | bytes 2359312 | tf_op jit(solution)/shard_map/all_gather | solution.py:123
  229.9 3.9 %convolution_convert_fusion = bf16[256,4608]{1,0:T(8,128)(2,1)} fusion(bf16[256,256]{0,1:T(8,128)(2,1)S(1)} %bitcast.59, bf16[256,4608]{0,1:T(8,128)(2,1)} %all-gather.16.cloned.1.call-done), kind=kOutput, calls=%fused_computation.21 | convolution fusion | flops 605159424 | bytes 4849664 | tf_op jit(solution)/shard_map/dot_general | solution.py:122
  233.9 54.4 %all-reduce.3.cloned.1.call-done = bf16[256,4608]{1,0:T(8,128)(2,1)} async-done(((bf16[256,4608]{1,0:T(8,128)(2,1)}), bf16[256,4608]{1,0:T(8,128)(2,1)}) %all-reduce.3.cloned.1.call-update) | async-done | bytes 2359312 | tf_op jit(solution)/shard_map/psum | solution.py:126
  288.2 2.4 fusion.12
  290.6 2.6 fusion.17
  (60 shorter events, 4.2 us)
Async XLA Ops:
  6.5 72.5 %copy-start.4 = (f32[4608]{0:T(1024)S(1)}, f32[4608]{0:T(1024)}, u32[]{:S(2)}) copy-start(f32[4608]{0:T(1024)} %param.14) | copy-start | bytes 55300
  6.5 31.0 %all-gather.8.cloned.1.call-start = ((), (), s32[]{:S(2)}) async-start(), calls=%async_computation | async-start | bytes 2949120 | tf_op jit(solution)/shard_map/all_gather | solution.py:48
  7.3 71.8 %all-gather.10.cloned.1.call-start = ((), (), s32[]{:S(2)}) async-start(), calls=%async_computation.1 | async-start | bytes 1327104 | tf_op jit(solution)/shard_map/all_gather | solution.py:55
  8.0 114.4 %all-gather.14.cloned.1.call-start = ((), (), s32[]{:S(2)}) async-start(), calls=%async_computation.3 | async-start | bytes 1327104 | tf_op jit(solution)/shard_map/all_gather | solution.py:56
  8.7 168.2 %all-gather.12.cloned.1.call-start = ((), (), s32[]{:S(2)}) async-start(), calls=%async_computation.2 | async-start | bytes 2654208 | tf_op jit(solution)/shard_map/all_gather | solution.py:54
  9.3 220.6 %all-gather.16.cloned.1.call-start = ((), (), s32[]{:S(2)}) async-start(), calls=%async_computation.4 | async-start | bytes 2654208 | tf_op jit(solution)/shard_map/all_gather | solution.py:123
  9.9 278.3 %all-reduce.3.cloned.1.call-start = ((), (), s32[]{:S(2)}) async-start(), calls=%async_computation.5 | async-start | bytes 4718592 | tf_op jit(solution)/shard_map/psum | solution.py:126
  37.5 41.5 %copy-start = (bf16[256,4608]{1,0:T(8,128)(2,1)S(1)}, bf16[256,4608]{1,0:T(8,128)(2,1)}, u32[]{:S(2)}) copy-start(bf16[256,4608]{1,0:T(8,128)(2,1)} %all-gather.8.cloned.1.call-done) | copy-start | bytes 7077892
  229.9 60.7 %copy-start.3 = (f32[4608]{0:T(1024)S(1)}, f32[4608]{0:T(1024)}, u32[]{:S(2)}) copy-start(f32[4608]{0:T(1024)} %param.15) | copy-start | bytes 55300
  233.9 56.8 %copy-start.1 = (bf16[256,4608]{1,0:T(8,128)(2,1)S(1)}, bf16[256,4608]{1,0:T(8,128)(2,1)}, u32[]{:S(2)}) copy-start(bf16[256,4608]{1,0:T(8,128)(2,1)} %all-gather.8.cloned.1.call-done) | copy-start | bytes 7077892
  288.2 2.4 copy-start.2
Sparse Core Ops, SparseCore 0:
  8.9 26.7 all-gather.7
  37.9 41.1 all-gather.9
  81.2 41.1 all-gather.13
  124.5 52.4 all-gather.11
  179.0 50.8 all-gather.15
  234.0 54.1 all-reduce.2
where the time goes:
time: 300 us
  waiting for transfers between devices  168 us (56%)
  blocking collectives  89.8 us (30%)
  matrix products  16.3 us (5%)
  between operations  14.3 us (5%)
  other arithmetic  9.87 us (3%)
    psum x1, waiting for transfers between devices, local(): lax.psum(partial_proj.astype(jnp.bfloat16), 'head').astype(jnp.float32)  54.4 us
    all_gather x1, waiting for transfers between devices, local(): lax.all_gather(w_out, 'seq', axis=1, tiled=True)  44.5 us
    all_gather x1, waiting for transfers between devices, local(): lax.all_gather(w_key, 'seq', axis=0, tiled=True)  39.1 us
    all_gather x1, blocking collectives, local(): keys_all = lax.all_gather(rk, 'seq', axis=0, tiled=True)  34.4 us
    all_gather x1, blocking collectives, local(): values_all = lax.all_gather(vb, 'seq', axis=0, tiled=True)  32.3 us
    unnamed x1, blocking collectives  23.1 us
    all_gather x1, waiting for transfers between devices, local(): lax.all_gather(w_query, 'seq', axis=0, tiled=True)  20 us
    dot_general x3, matrix products, local(): jnp.dot(normed, piece, preferred_element_type=jnp.float32)  7.5 us
  transfers between devices with their start and end apart: 6, of which 5 were waited for; matrix products, arithmetic and copies ran while one was open for 6% of the time, Pallas kernels for 0%

commit v1 on v0

--- a/solution.py
+++ b/solution.py
@@ -2,6 +2,7 @@
 import jax.numpy as jnp
 from jax import lax
 from jax.sharding import PartitionSpec as P
+from jax.lax import all_gather
 
 HD = 128
 GROUP = 2
@@ -82,8 +83,11 @@
         jnp.zeros((kv_count, GROUP * rows, HD), jnp.float32),
         jnp.zeros((kv_count, GROUP * rows), jnp.float32),
     )
-    keys_all = lax.all_gather(rk, "seq", axis=0, tiled=True)
-    values_all = lax.all_gather(vb, "seq", axis=0, tiled=True)
+    keys_all, values_all = jnp.split(
+        all_gather(jnp.concatenate([rk, vb], axis=1), "seq", tiled=True, axis=0),
+        [rk.shape[1]],
+        axis=1,
+    )
     count = keys_all.shape[0]
     block = 1024
     steps_total = count // block

time: 300 us -> 337 us (1.12)
  waiting for transfers between devices: 168 us -> 270 us
  blocking collectives: 89.8 us -> 23.1 us
    all_gather x2 -> x0, blocking collectives: 66.7 us -> none  [the longest x1 34.4 us: local(): keys_all = lax.all_gather(rk, 'seq', axis=0, tiled=True)]
    all_gather x0 -> x1, waiting for transfers between devices: none -> 36.7 us  [local(): all_gather(jnp.concatenate([rk, vb], axis=1), 'seq', tiled=True, axis=0)]
    all_gather x1, waiting for transfers between devices: 6.33 us -> 39.4 us  [local(): lax.all_gather(w_value, 'seq', axis=0, tiled=True)]
    all_gather x1, waiting for transfers between devices: 20 us -> 48.6 us  [local(): lax.all_gather(w_query, 'seq', axis=0, tiled=True)]
    all_gather x1, waiting for transfers between devices: 44.5 us -> 48.2 us  [local(): lax.all_gather(w_out, 'seq', axis=1, tiled=True)]
  transfers between devices with their start and end apart: 6 -> 7, of which waited for: 5 -> 6; matrix products, arithmetic and copies ran while one was open for 6% -> 6% of each run, Pallas kernels for 0% -> 0%
where the time goes in v1:
time: 337 us
  waiting for transfers between devices  270 us (80%)
  blocking collectives  23.1 us (7%)
  matrix products  14.4 us (4%)
  between operations  14.3 us (4%)
  other arithmetic  10.5 us (3%)
    psum x1, waiting for transfers between devices, local(): lax.psum(partial_proj.astype(jnp.bfloat16), 'head').astype(jnp.float32)  54.3 us
    all_gather x1, waiting for transfers between devices, local(): lax.all_gather(w_query, 'seq', axis=0, tiled=True)  48.6 us
    all_gather x1, waiting for transfers between devices, local(): lax.all_gather(w_out, 'seq', axis=1, tiled=True)  48.2 us
    all_gather x1, waiting for transfers between devices, local(): lax.all_gather(w_key, 'seq', axis=0, tiled=True)  40.1 us
    all_gather x1, waiting for transfers between devices, local(): lax.all_gather(w_value, 'seq', axis=0, tiled=True)  39.4 us
    all_gather x1, waiting for transfers between devices, local(): all_gather(jnp.concatenate([rk, vb], axis=1), 'seq', tiled=True, axis=0)  36.7 us
    unnamed x1, blocking collectives  23.1 us
    dot_general x3, matrix products, local(): jnp.dot(normed, piece, preferred_element_type=jnp.float32)  7.56 us
  transfers between devices with their start and end apart: 7, of which 6 were waited for; matrix products, arithmetic and copies ran while one was open for 6% of the time, Pallas kernels for 0%

profile of v1, /device:TPU:0, one launch (start us, length us, event | category | flops | bytes accessed | tf_op | source)
XLA Modules:
  0.0 336.5 jit_solution(11181062297098965598)
XLA Ops:
  6.5 0.7 all-gather.8.cloned.1.call-update
  7.3 0.7 all-gather.10.cloned.1.call-update
  8.1 0.7 all-gather.12.cloned.1.call-update
  9.4 1.2 dynamic-slice
  11.3 0.8 convert_reduce_fusion
  12.3 23.1 %all-reduce = f32[64]{0:T(128)S(1)} all-reduce(f32[64]{0:T(128)S(1)} %dynamic-update-slice), channel_id=2, replica_groups=mesh['seq'=8,'head'=4] {'seq'}, use_global_device_ids=true, to_apply=%add | all-reduce | flops 64 | bytes 512
  35.8 0.8 select_reduce_fusion
  36.6 2.4 fusion.14
  39.0 40.1 %all-gather.10.cloned.1.call-done = bf16[4608,128]{1,0:T(8,128)(2,1)} async-done(((bf16[576,128]{1,0:T(8,128)(2,1)}), bf16[4608,128]{1,0:T(8,128)(2,1)}) %all-gather.10.cloned.1.call-update) | async-done | bytes 1179664 | tf_op jit(solution)/shard_map/all_gather | solution.py:56
  79.0 2.3 convolution_bitcast_fusion.1
  81.7 39.4 %all-gather.12.cloned.1.call-done = bf16[4608,128]{1,0:T(8,128)(2,1)} async-done(((bf16[576,128]{1,0:T(8,128)(2,1)}), bf16[4608,128]{1,0:T(8,128)(2,1)}) %all-gather.12.cloned.1.call-update) | async-done | bytes 1179664 | tf_op jit(solution)/shard_map/all_gather | solution.py:57
  121.1 2.3 convolution_convert_fusion.1
  125.1 48.6 %all-gather.16.cloned.1.call-done = bf16[4608,256]{1,0:T(8,128)(2,1)} async-done(((bf16[576,256]{1,0:T(8,128)(2,1)}), bf16[4608,256]{1,0:T(8,128)(2,1)}) %all-gather.16.cloned.1.call-update) | async-done | bytes 2359312 | tf_op jit(solution)/shard_map/all_gather | solution.py:55
  173.6 2.9 fusion.29
  176.8 36.7 %all-gather.14.cloned.1.call-done = bf16[2048,256]{0,1:T(8,128)(2,1)} async-done(((bf16[256,256]{0,1:T(8,128)(2,1)}), bf16[2048,256]{0,1:T(8,128)(2,1)}) %all-gather.14.cloned.1.call-update) | async-done | bytes 1048592 | tf_op jit(solution)/shard_map/all_gather | solution.py:87
  213.5 1.3 fusion.34
  214.8 3.1 while.31
  214.9 1.0 fusion.48
  216.4 1.0 fusion.48
  218.2 48.2 %all-gather.18.cloned.1.call-done = bf16[256,4608]{0,1:T(8,128)(2,1)} async-done(((bf16[256,576]{0,1:T(8,128)(2,1)}), bf16[256,4608]{0,1:T(8,128)(2,1)}) %all-gather.18.cloned.1.call-update) | async-done | bytes 2359312 | tf_op jit(solution)/shard_map/all_gather | solution.py:127
  266.4 3.9 %convolution_convert_fusion = bf16[256,4608]{1,0:T(8,128)(2,1)} fusion(bf16[256,256]{0,1:T(8,128)(2,1)S(1)} %bitcast.60, bf16[256,4608]{0,1:T(8,128)(2,1)} %all-gather.18.cloned.1.call-done), kind=kOutput, calls=%fused_computation.21 | convolution fusion | flops 605159424 | bytes 4849664 | tf_op jit(solution)/shard_map/dot_general | solution.py:126
  270.4 54.3 %all-reduce.3.cloned.1.call-done = bf16[256,4608]{1,0:T(8,128)(2,1)} async-done(((bf16[256,4608]{1,0:T(8,128)(2,1)}), bf16[256,4608]{1,0:T(8,128)(2,1)}) %all-reduce.3.cloned.1.call-update) | async-done | bytes 2359312 | tf_op jit(solution)/shard_map/psum | solution.py:130
  324.7 2.4 fusion.12
  327.1 2.6 fusion.17
  (63 shorter events, 4.9 us)
Async XLA Ops:
  6.5 72.5 %copy-start.4 = (f32[4608]{0:T(1024)S(1)}, f32[4608]{0:T(1024)}, u32[]{:S(2)}) copy-start(f32[4608]{0:T(1024)} %param.14) | copy-start | bytes 55300
  6.5 30.0 %all-gather.8.cloned.1.call-start = ((), (), s32[]{:S(2)}) async-start(), calls=%async_computation | async-start | bytes 2949120 | tf_op jit(solution)/shard_map/all_gather | solution.py:49
  7.3 71.8 %all-gather.10.cloned.1.call-start = ((), (), s32[]{:S(2)}) async-start(), calls=%async_computation.1 | async-start | bytes 1327104 | tf_op jit(solution)/shard_map/all_gather | solution.py:56
  8.0 113.1 %all-gather.12.cloned.1.call-start = ((), (), s32[]{:S(2)}) async-start(), calls=%async_computation.2 | async-start | bytes 1327104 | tf_op jit(solution)/shard_map/all_gather | solution.py:57
  8.7 164.9 %all-gather.16.cloned.1.call-start = ((), (), s32[]{:S(2)}) async-start(), calls=%async_computation.4 | async-start | bytes 2654208 | tf_op jit(solution)/shard_map/all_gather | solution.py:55
  9.3 204.2 %all-gather.14.cloned.1.call-start = ((), (), s32[]{:S(2)}) async-start(), calls=%async_computation.3 | async-start | bytes 1179648 | tf_op jit(solution)/shard_map/all_gather | solution.py:87
  36.6 42.4 %copy-start = (bf16[256,4608]{1,0:T(8,128)(2,1)S(1)}, bf16[256,4608]{1,0:T(8,128)(2,1)}, u32[]{:S(2)}) copy-start(bf16[256,4608]{1,0:T(8,128)(2,1)} %all-gather.8.cloned.1.call-done) | copy-start | bytes 7077892
  124.1 142.3 %all-gather.18.cloned.1.call-start = ((), (), s32[]{:S(2)}) async-start(), calls=%async_computation.5 | async-start | bytes 2654208 | tf_op jit(solution)/shard_map/all_gather | solution.py:127
  124.7 200.0 %all-reduce.3.cloned.1.call-start = ((), (), s32[]{:S(2)}) async-start(), calls=%async_computation.6 | async-start | bytes 4718592 | tf_op jit(solution)/shard_map/psum | solution.py:130
  266.4 60.7 %copy-start.3 = (f32[4608]{0:T(1024)S(1)}, f32[4608]{0:T(1024)}, u32[]{:S(2)}) copy-start(f32[4608]{0:T(1024)} %param.15) | copy-start | bytes 55300
  270.3 56.8 %copy-start.1 = (bf16[256,4608]{1,0:T(8,128)(2,1)S(1)}, bf16[256,4608]{1,0:T(8,128)(2,1)}, u32[]{:S(2)}) copy-start(bf16[256,4608]{1,0:T(8,128)(2,1)} %all-gather.8.cloned.1.call-done) | copy-start | bytes 7077892
  324.7 2.4 copy-start.2
Sparse Core Ops, SparseCore 0:
  8.9 26.7 all-gather.7
  37.9 41.1 all-gather.9
  81.2 39.8 all-gather.11
  123.1 50.4 all-gather.15
  175.5 37.9 all-gather.13
  215.5 50.8 all-gather.17
  270.5 54.1 all-reduce.2
